TPU v7x, 32 devices: a whole 2x2x4 slice. The times are simulated.
32 devices in a mesh: wide: 4 (over y, x), narrow: 8 (over z, core).
Axes of the slice: x: 2, y: 2, z: 4, core: 2. Of those that a mesh axis runs over, the one named last changes fastest.
Arguments:
- charges: bfloat16 [512, 256, 128], P(('wide', 'narrow')), may hold values from -6 to 6
- pairs_first: int32 [2048, 4], P(('wide', 'narrow')), may hold values from 0 to 15, as said below
- pairs_second: int32 [2048, 4], P(('wide', 'narrow')), may hold values from 0 to 15, as said below
- pairs_third: int32 [2048, 4], P(('wide', 'narrow')), may hold values from 0 to 15, as said below
- matrices_first: bfloat16 [256, 256, 256], P(('wide', 'narrow')), may hold values from -0.21875 to 0.21875
- matrices_second: bfloat16 [256, 256, 256], P(('wide', 'narrow')), may hold values from -0.21875 to 0.21875
- matrices_third: bfloat16 [256, 256, 256], P(('wide', 'narrow')), may hold values from -0.21875 to 0.21875
- box_owner: int32 [4, 8, 16], P('wide', 'narrow'), may hold values from 0 to 3, as said below
Outputs:
- potentials: bfloat16 [512, 256, 128], P(('wide', 'narrow'))
Inputs may be any that keep to these rules, and one draw needn't show every extreme that they name: `pairs_first`: each device's 64 rows hold a source box and a target box below 16, a matrix below 8 and a live flag 0 or 1; live rows come before the others; in every list some device has all rows live. `pairs_second`: same form as pairs_first. `pairs_third`: same form as pairs_first. `box_owner`: for each narrow index, every wide index hands 0 or 8 of its boxes to each owner, and each owner receives exactly 16 boxes.
All inputs are finite; a program needn't handle non-finite values.
Results may differ from a plain program's by a relative error of at most 0.0057.
Values may be sent and summed in bfloat16 or wider, within the bound.
No kernel may reach another device: no remote copies, remote signals or barrier semaphores. Data moves between devices by JAX's collectives and lax.ppermute only.
A program may use at most 64 MiB of HBM per device.

v0:
```python
import functools

import jax
import jax.numpy as jnp
from jax import lax
from jax.experimental import pallas as pl
from jax.experimental.pallas import tpu as pltpu
from jax.sharding import PartitionSpec as P


UNROLL = 16
PARTS = 4
GRANT = pltpu.CompilerParams(vmem_limit_bytes=16 * 2**20)
VMEM = pl.BlockSpec(memory_space=pltpu.VMEM)
SMEM = pl.BlockSpec(memory_space=pltpu.SMEM)
HBM = pl.BlockSpec(memory_space=pltpu.HBM)


def steps(size):
    top = size // 2
    far, near = list(range(top, size)), list(range(2, top))
    return far[: top // 2] + near + far[top // 2 :] + list(range(1, min(2, top))) + [0]


def left_half(shape):
    return lax.broadcasted_iota(jnp.int32, shape, len(shape) - 1) < shape[-1] // 2


def swap(block):
    return pltpu.roll(block, block.shape[-1] // 2, block.ndim - 1)


def live_count(pairs):
    count = pairs[3, 0]
    for row in range(1, pairs.shape[1]):
        count = count + pairs[3, row]
    return count


def accumulate(pairs, mats, source, place, acc):
    dummy = acc.shape[0] - 1

    def group(index, carry):
        products = []
        for step in range(UNROLL):
            row = index * UNROLL + step
            slot, half = place(pairs[1, row])
            slot = jnp.where(pairs[3, row] > 0, slot, dummy)
            product = jnp.dot(
                mats[pairs[2, row]], source(pairs[0, row], half),
                preferred_element_type=jnp.float32,
            )
            products.append((slot, product))
        for slot, product in products:
            acc[slot] += product
        return carry

    lax.fori_loop(0, (live_count(pairs) + UNROLL - 1) // UNROLL, group, 0)


def clear(acc):
    def one(index, carry):
        acc[index] = jnp.zeros(acc.shape[1:], acc.dtype)
        return carry

    lax.fori_loop(0, acc.shape[0], one, 0)


def fetch(source, target, sems, parts):
    size = source.shape[0] // parts
    copies = [
        pltpu.make_async_copy(
            source.at[pl.ds(p * size, size)], target.at[pl.ds(p * size, size)], sems.at[p]
        )
        for p in range(parts)
    ]
    for copy in copies:
        copy.start()

    def wait():
        for copy in copies:
            copy.wait()

    return wait


def first_kernel(size, pairs_hbm, charges_hbm, mats_hbm, *refs):
    count = 2 * size - 2
    outs, (acc, pairs, charges, mats, sems) = refs[:count], refs[count:]
    waits = [
        fetch(pairs_hbm, pairs, sems.at[0], 1),
        fetch(charges_hbm, charges, sems.at[1], PARTS),
        fetch(mats_hbm, mats, sems.at[2], PARTS),
    ]
    me = lax.axis_index("narrow")
    boxes, width, columns = charges.shape
    piece = width // size
    clear(acc)
    for wait in waits:
        wait()
    accumulate(
        pairs, mats, lambda s, half: charges[s], lambda k: (k, 0), acc
    )
    left = left_half((piece, columns))
    half, far = boxes // 2, size - 2
    for at, r in enumerate(steps(size)):
        rows = pl.ds(pl.multiple_of((me ^ r) * piece, piece), piece)
        targets = (outs[at], outs[far + at]) if at < far else (
            outs[far + at].at[pl.ds(0, half)], outs[far + at].at[pl.ds(half, half)]
        )

        def one(i, carry, targets=targets, rows=rows):
            a = acc[2 * i, rows, :]
            b = acc[2 * i + 1, rows, :]
            targets[0][i] = jnp.where(left, a, swap(b)).astype(jnp.bfloat16)
            targets[1][i] = jnp.where(left, swap(a), b).astype(jnp.bfloat16)
            return carry

        lax.fori_loop(0, half, one, 0, unroll=True)


def assemble(me, ins, view):
    count, piece, columns = ins[0].shape
    left = left_half((piece, columns))
    nothing = jnp.zeros((piece, columns), jnp.bfloat16)
    for r, ref in zip(steps(len(ins)), ins):
        rows = pl.ds(pl.multiple_of((me ^ r) * piece, piece), piece)
        for i in range(count):
            block = ref[i]
            turned = swap(block)
            view[4 * i, rows, :] = jnp.where(left, block, nothing)
            view[4 * i + 1, rows, :] = jnp.where(left, nothing, turned)
            view[4 * i + 2, rows, :] = jnp.where(left, turned, nothing)
            view[4 * i + 3, rows, :] = jnp.where(left, nothing, block)


def second_kernel(narrow, wide, chunk, pairs_hbm, mats, *refs):
    ins, outs = refs[:narrow], refs[narrow : narrow + wide]
    count = outs[0].shape[0]
    ins = [*ins[:-2], *(near.at[pl.ds(chunk * count, count)] for near in ins[-2:])]
    acc, view, pairs, sems = refs[narrow + wide :]
    wait = fetch(pairs_hbm, pairs, sems.at[0], 1)
    me = lax.axis_index("wide")
    count, piece, _ = outs[0].shape
    assemble(lax.axis_index("narrow"), ins, view)
    clear(acc)
    wait()
    accumulate(
        pairs, mats, lambda s, half: view[2 * s + half],
        lambda k: (k >> 1, k & 1), acc,
    )
    for at, r in enumerate(steps(wide)):
        rows = pl.ds(pl.multiple_of((me ^ r) * piece, piece), piece)
        for i in range(count):
            outs[at][i] = acc[i, rows, :].astype(jnp.bfloat16)


def third_kernel(wide, owners_hbm, pairs_hbm, mats, *refs):
    ins, outs = refs[:wide], refs[wide : 2 * wide]
    acc, view, filled, spots, owners, pairs, sems = refs[2 * wide :]
    wait = fetch(pairs_hbm, pairs, sems.at[0], 1)
    wait_owners = fetch(owners_hbm, owners, sems.at[1], 1)
    boxes = owners.shape[1]
    width, columns = acc.shape[1:]
    room = 2 * boxes // wide
    me = lax.axis_index("wide")
    assemble(me, ins, view)
    clear(acc)
    wait_owners()
    for o in range(wide):
        filled[o] = 0
    for k in range(boxes):
        o = owners[0, k]
        spots[k] = o * room + filled[o]
        filled[o] = filled[o] + 1
    wait()
    accumulate(
        pairs, mats, lambda s, half: view[2 * s + half],
        lambda k: (spots[k] >> 1, spots[k] & 1), acc,
    )
    for at, r in enumerate(steps(wide)):
        o = me ^ r
        flag = (filled[o] > 0).astype(jnp.float32)
        for p in range(room // 2):
            outs[at][pl.ds(p * width, width), :] = acc[o * (room // 2) + p].astype(jnp.bfloat16)
        tail = outs[at].shape[0] - room // 2 * width
        outs[at][pl.ds(room // 2 * width, tail), :] = jnp.full(
            (tail, columns), flag, jnp.float32
        ).astype(jnp.bfloat16)


def last_kernel(wide, *refs):
    ins, out, flags = refs[: 2 * wide], refs[2 * wide], refs[2 * wide + 1]
    boxes, width, columns = out.shape
    room = 2 * boxes // wide
    me = lax.axis_index("wide")
    for at, r in enumerate(steps(wide)):
        mark = ins[at][pl.ds(room // 2 * width, 16), :].astype(jnp.float32)
        flags[me ^ r] = (jnp.max(mark) > 0.5).astype(jnp.int32)
    left = left_half((width, columns))
    for at, r in enumerate(steps(wide)):
        origin = me ^ r
        base = jnp.int32(0)
        for w in range(wide):
            base = base + jnp.where(w < origin, flags[w], 0) * room

        @pl.when(flags[origin] > 0)
        def _(at=at, base=base):
            for p in range(room // 2):
                a = ins[at][pl.ds(p * width, width), :]
                b = ins[wide + at][pl.ds(p * width, width), :]
                out[base + 2 * p] = jnp.where(left, a, swap(b))
                out[base + 2 * p + 1] = jnp.where(left, swap(a), b)


def exchange(parts, axis, size, order):
    moved = []
    for r, part in zip(order, parts):
        moved.append(lax.ppermute(part, axis, [(i, i ^ r) for i in range(size)]) if r else part)
    return moved


def cost(pair_count, width, columns, moved):
    return pl.CostEstimate(
        flops=2 * pair_count * width * width * columns, bytes_accessed=moved, transcendentals=0
    )


def per_device(
    narrow, wide, charges, pairs_first, pairs_second, pairs_third,
    matrices_first, matrices_second, matrices_third, box_owner,
):
    boxes, width, columns = charges.shape
    half = boxes // 2
    room = 2 * boxes // wide
    pair_count = pairs_first.shape[0]
    pairs_first, pairs_second, pairs_third = [
        pltpu.with_memory_space_constraint(x.T, pltpu.HBM)
        for x in (pairs_first, pairs_second, pairs_third)
    ]
    owners = pltpu.with_memory_space_constraint(box_owner.reshape(1, boxes), pltpu.HBM)
    estimate = cost(pair_count, width, columns, 4 * boxes * width * columns)

    def blocks(shape, count):
        return [jax.ShapeDtypeStruct(shape, jnp.bfloat16)] * count

    far = narrow - 2
    sent = pl.pallas_call(
        functools.partial(first_kernel, narrow),
        out_shape=blocks((half, width // narrow, columns), 2 * far)
        + blocks((2 * half, width // narrow, columns), narrow - far),
        in_specs=[HBM] * 3,
        out_specs=[VMEM] * (narrow + far),
        scratch_shapes=[
            pltpu.VMEM((boxes + 1, width, columns), jnp.float32),
            pltpu.SMEM(pairs_first.shape, jnp.int32),
            pltpu.VMEM(charges.shape, charges.dtype),
            pltpu.VMEM(matrices_first.shape, matrices_first.dtype),
            pltpu.SemaphoreType.DMA((3, PARTS)),
        ],
        cost_estimate=estimate,
        compiler_params=GRANT,
        name="first_level",
    )(*[pltpu.with_memory_space_constraint(x, pltpu.HBM) for x in (pairs_first, charges, matrices_first)])

    view = pltpu.VMEM((2 * boxes, width, columns), jnp.bfloat16)
    listed = [pltpu.SMEM(pairs_first.shape, jnp.int32), pltpu.SemaphoreType.DMA((2, 1))]
    second = lambda chunk: pl.pallas_call(
        functools.partial(second_kernel, narrow, wide, chunk),
        out_shape=blocks((half, width // wide, columns), wide),
        in_specs=[HBM, VMEM] + [VMEM] * narrow,
        out_specs=[VMEM] * wide,
        scratch_shapes=[pltpu.VMEM((half + 1, width, columns), jnp.float32), view, *listed],
        cost_estimate=estimate,
        compiler_params=GRANT,
        name="second_level",
    )
    third = pl.pallas_call(
        functools.partial(third_kernel, wide),
        out_shape=blocks((room // 2 * width + 16, columns), wide),
        in_specs=[HBM, HBM, VMEM] + [VMEM] * wide,
        out_specs=[VMEM] * wide,
        scratch_shapes=[
            pltpu.VMEM((wide * room // 2 + 1, width, columns), jnp.float32), view,
            pltpu.SMEM((wide,), jnp.int32), pltpu.SMEM((boxes,), jnp.int32),
            pltpu.SMEM((1, boxes), jnp.int32), *listed,
        ],
        cost_estimate=estimate,
        compiler_params=GRANT,
        name="third_level",
    )
    order = steps(narrow)
    first_far = exchange(sent[:far], "narrow", narrow, order[:far])
    near = exchange(sent[2 * far :], "narrow", narrow, order[far:])
    second_far = exchange(sent[far : 2 * far], "narrow", narrow, order[:far])
    moved = [
        exchange(
            second(chunk)(pairs_second, matrices_second, *parts, *near),
            "wide", wide, steps(wide),
        )
        for chunk, parts in enumerate((first_far, second_far))
    ]
    moved = [
        exchange(
            third(owners, pairs_third, matrices_third, *parts),
            "wide", wide, steps(wide),
        )
        for parts in moved
    ]
    return pl.pallas_call(
        functools.partial(last_kernel, wide),
        out_shape=jax.ShapeDtypeStruct((boxes, width, columns), jnp.bfloat16),
        in_specs=[VMEM] * (2 * wide),
        out_specs=VMEM,
        scratch_shapes=[pltpu.SMEM((wide,), jnp.int32)],
        compiler_params=GRANT,
        name="place",
    )(*moved[0], *moved[1])


def solution(mesh):
    narrow, wide = mesh.shape["narrow"], mesh.shape["wide"]
    rows = P(("wide", "narrow"), None)
    blocks = P(("wide", "narrow"), None, None)

    def body(*arrays):
        return per_device(narrow, wide, *arrays)

    return jax.shard_map(
        body,
        mesh=mesh,
        in_specs=(blocks, rows, rows, rows, blocks, blocks, blocks, P("wide", "narrow", None)),
        out_specs=blocks,
        check_vma=False,
    )
```

profile of v0, /device:TPU:0, one launch (start us, length us, event | category | flops | bytes accessed | tf_op | source)
XLA Modules:
  0.0 84.4 jit_solution(14755753504845626938)
XLA Ops:
  0.0 4.9 %first_level.1 = (bf16[8,32,128]{2,1,0:T(8,128)(2,1)S(1)}, bf16[8,32,128]{2,1,0:T(8,128)(2,1)S(1)}, bf16[8,32,128]{2,1,0:T(8,128)(2,1)S(1)}, bf16[8,32,128]{2,1,...) custom-call(s32[4,64]{1,0:T(4,128)} %bitcast.4, ...), custom_call_target="tpu_custom_call" | custom-call | flops 1073741824 | bytes 2097152 | tf_op jit(solution)/shard_map/first_level/pallas_call | solution.py:248
  4.9 2.7 %collective-permute-start = (bf16[8,32,128]{2,1,0:T(8,128)(2,1)S(1)}, bf16[8,32,128]{2,1,0:T(8,128)(2,1)S(1)}, u32[]{:S(2)}, u32[]{:S(2)}) collective-permute-start(bf16[8,32,128]{2,1,0:T(8,128)(2,1)S(1)} %get-tuple-element.35), channel_id=1, source_target_pairs={{0,4},{1,5},{2,6},{3,7},{4,0},{5,1},{6,2},{7,3},{8,12},{9,13},{10,... | collective-permute-start | bytes 196616 | tf_op jit(solution)/shard_map/ppermute | solution.py:219
  8.0 3.1 %collective-permute-start.2 = (bf16[8,32,128]{2,1,0:T(8,128)(2,1)S(1)}, bf16[8,32,128]{2,1,0:T(8,128)(2,1)S(1)}, u32[]{:S(2)}, u32[]{:S(2)}) collective-permute-start(bf16[8,32,128]{2,1,0:T(8,128)(2,1)S(1)} %get-tuple-element.37), channel_id=1, source_target_pairs={{0,2},{1,3},{2,0},{3,1},{4,6},{5,7},{6,4},{7,5},{8,10},{9,11},{10,... | collective-permute-start | bytes 196616 | tf_op jit(solution)/shard_map/ppermute | solution.py:219
  11.1 5.2 %collective-permute-start.4 = (bf16[8,32,128]{2,1,0:T(8,128)(2,1)S(1)}, bf16[8,32,128]{2,1,0:T(8,128)(2,1)S(1)}, u32[]{:S(2)}, u32[]{:S(2)}) collective-permute-start(bf16[8,32,128]{2,1,0:T(8,128)(2,1)S(1)} %get-tuple-element.39), channel_id=1, source_target_pairs={{0,6},{1,7},{2,4},{3,5},{4,2},{5,3},{6,0},{7,1},{8,14},{9,15},{10,... | collective-permute-start | bytes 196616 | tf_op jit(solution)/shard_map/ppermute | solution.py:219
  16.8 1.7 %collective-permute-done.4.refs_4_ = bf16[8,32,128]{2,1,0:T(8,128)(2,1)S(1)} collective-permute-done((bf16[8,32,128]{2,1,0:T(8,128)(2,1)S(1)}, bf16[8,32,128]{2,1,0:T(8,128)(2,1)S(1)}, u32[]{:S(2)}, u32[]{:S(2)}) %collective-permute-start.4) | collective-permute-done | bytes 65568 | tf_op jit(solution)/shard_map/ppermute | solution.py:219
  18.6 3.1 %collective-permute-done.5.refs_5_ = bf16[8,32,128]{2,1,0:T(8,128)(2,1)S(1)} collective-permute-done((bf16[8,32,128]{2,1,0:T(8,128)(2,1)S(1)}, bf16[8,32,128]{2,1,0:T(8,128)(2,1)S(1)}, u32[]{:S(2)}, u32[]{:S(2)}) %collective-permute-start.5) | collective-permute-done | bytes 65568 | tf_op jit(solution)/shard_map/ppermute | solution.py:219
  21.7 1.9 %second_level.2 = (bf16[8,64,128]{2,1,0:T(8,128)(2,1)S(1)}, bf16[8,64,128]{2,1,0:T(8,128)(2,1)S(1)}, bf16[8,64,128]{2,1,0:T(8,128)(2,1)S(1)}, bf16[8,64,128]{2,1,0:T(8,128)(2,1)S(1)}) custom-call(s32[4,64]{1,0:T(4,128)} %bitcast.5, bf16[8,256,256]{2,1,0:T(8,128)(2,1)S(1)} %copy-done, bf16[8,32,128]{2,1,0:T(8,128)(2,1)S(1)} %collective-permute-done.refs_0_, ...), custom_call_target="tpu_custom_call" | custom-call | flops 1073741824 | bytes 2097152 | tf_op jit(solution)/shard_map/second_level/pallas_call | solution.py:298
  23.6 4.6 %collective-permute-start.7 = (bf16[8,64,128]{2,1,0:T(8,128)(2,1)S(1)}, bf16[8,64,128]{2,1,0:T(8,128)(2,1)S(1)}, u32[]{:S(2)}, u32[]{:S(2)}) collective-permute-start(bf16[8,64,128]{2,1,0:T(8,128)(2,1)S(1)} %get-tuple-element.43), channel_id=1, source_target_pairs={{0,16},{8,24},{16,0},{24,8},{1,17},{9,25},{17,1},{25,9},{2,18},{10... | collective-permute-start | bytes 393224 | tf_op jit(solution)/shard_map/ppermute | solution.py:219
  29.8 2.1 %collective-permute-start.14 = (bf16[8,32,128]{2,1,0:T(8,128)(2,1)S(1)}, bf16[8,32,128]{2,1,0:T(8,128)(2,1)S(1)}, u32[]{:S(2)}, u32[]{:S(2)}) collective-permute-start(bf16[8,32,128]{2,1,0:T(8,128)(2,1)S(1)} %get-tuple-element.52), channel_id=1, source_target_pairs={{0,5},{1,4},{2,7},{3,6},{4,1},{5,0},{6,3},{7,2},{8,13},{9,12},{10,... | collective-permute-start | bytes 196616 | tf_op jit(solution)/shard_map/ppermute | solution.py:219
  31.9 5.1 %collective-permute-done.13.refs_0_ = bf16[8,32,128]{2,1,0:T(8,128)(2,1)S(1)} collective-permute-done((bf16[8,32,128]{2,1,0:T(8,128)(2,1)S(1)}, bf16[8,32,128]{2,1,0:T(8,128)(2,1)S(1)}, u32[]{:S(2)}, u32[]{:S(2)}) %collective-permute-start.13) | collective-permute-done | bytes 65568 | tf_op jit(solution)/shard_map/ppermute | solution.py:219
  37.0 1.8 %collective-permute-start.17 = (bf16[8,32,128]{2,1,0:T(8,128)(2,1)S(1)}, bf16[8,32,128]{2,1,0:T(8,128)(2,1)S(1)}, u32[]{:S(2)}, u32[]{:S(2)}) collective-permute-start(bf16[8,32,128]{2,1,0:T(8,128)(2,1)S(1)} %get-tuple-element.55), channel_id=1, source_target_pairs={{0,6},{1,7},{2,4},{3,5},{4,2},{5,3},{6,0},{7,1},{8,14},{9,15},{10,... | collective-permute-start | bytes 196616 | tf_op jit(solution)/shard_map/ppermute | solution.py:219
  38.9 3.4 %collective-permute-start.18 = (bf16[8,32,128]{2,1,0:T(8,128)(2,1)S(1)}, bf16[8,32,128]{2,1,0:T(8,128)(2,1)S(1)}, u32[]{:S(2)}, u32[]{:S(2)}) collective-permute-start(bf16[8,32,128]{2,1,0:T(8,128)(2,1)S(1)} %get-tuple-element.56), channel_id=1, source_target_pairs={{0,7},{1,6},{2,5},{3,4},{4,3},{5,2},{6,1},{7,0},{8,15},{9,14},{10,... | collective-permute-start | bytes 196616 | tf_op jit(solution)/shard_map/ppermute | solution.py:219
  42.3 3.4 %third_level.2 = (bf16[1040,128]{1,0:T(8,128)(2,1)S(1)}, bf16[1040,128]{1,0:T(8,128)(2,1)S(1)}, bf16[1040,128]{1,0:T(8,128)(2,1)S(1)}, bf16[1040,128]{1,0:T(8,128)(2,1)S(1)}) custom-call(s32[1,16]{1,0:T(1,128)} %bitcast.9, s32[4,64]{1,0:T(4,128)} %bitcast.7, bf16[8,256,256]{2,1,0:T(8,128)(2,1)S(1)} %copy-done.1, ...), custom_call_target="tpu_custom_call" | custom-call | flops 1073741824 | bytes 2097152 | tf_op jit(solution)/shard_map/third_level/pallas_call | solution.py:305
  45.8 2.4 %collective-permute-start.10 = (bf16[1040,128]{1,0:T(8,128)(2,1)S(1)}, bf16[1040,128]{1,0:T(8,128)(2,1)S(1)}, u32[]{:S(2)}, u32[]{:S(2)}) collective-permute-start(bf16[1040,128]{1,0:T(8,128)(2,1)S(1)} %get-tuple-element.47), channel_id=1, source_target_pairs={{0,16},{8,24},{16,0},{24,8},{1,17},{9,25},{17,1},{25,9},{2,18},{10... | collective-permute-start | bytes 798728 | tf_op jit(solution)/shard_map/ppermute | solution.py:219
  48.2 1.8 %second_level.3 = (bf16[8,64,128]{2,1,0:T(8,128)(2,1)S(1)}, bf16[8,64,128]{2,1,0:T(8,128)(2,1)S(1)}, bf16[8,64,128]{2,1,0:T(8,128)(2,1)S(1)}, bf16[8,64,128]{2,1,0:T(8,128)(2,1)S(1)}) custom-call(s32[4,64]{1,0:T(4,128)} %bitcast.6, bf16[8,256,256]{2,1,0:T(8,128)(2,1)S(1)} %copy-done, bf16[8,32,128]{2,1,0:T(8,128)(2,1)S(1)} %collective-permute-done.13.refs_0_, ...), custom_call_target="tpu_custom_call" | custom-call | flops 1073741824 | bytes 2097152 | tf_op jit(solution)/shard_map/second_level/pallas_call | solution.py:298
  50.0 2.3 %collective-permute-start.19 = (bf16[8,64,128]{2,1,0:T(8,128)(2,1)S(1)}, bf16[8,64,128]{2,1,0:T(8,128)(2,1)S(1)}, u32[]{:S(2)}, u32[]{:S(2)}) collective-permute-start(bf16[8,64,128]{2,1,0:T(8,128)(2,1)S(1)} %get-tuple-element.57), channel_id=1, source_target_pairs={{0,16},{8,24},{16,0},{24,8},{1,17},{9,25},{17,1},{25,9},{2,18},{10... | collective-permute-start | bytes 393224 | tf_op jit(solution)/shard_map/ppermute | solution.py:219
  52.4 2.7 %collective-permute-start.20 = (bf16[8,64,128]{2,1,0:T(8,128)(2,1)S(1)}, bf16[8,64,128]{2,1,0:T(8,128)(2,1)S(1)}, u32[]{:S(2)}, u32[]{:S(2)}) collective-permute-start(bf16[8,64,128]{2,1,0:T(8,128)(2,1)S(1)} %get-tuple-element.58), channel_id=1, source_target_pairs={{0,24},{8,16},{16,8},{24,0},{1,25},{9,17},{17,9},{25,1},{2,26},{10... | collective-permute-start | bytes 393224 | tf_op jit(solution)/shard_map/ppermute | solution.py:219
  58.2 3.4 %collective-permute-start.12 = (bf16[1040,128]{1,0:T(8,128)(2,1)S(1)}, bf16[1040,128]{1,0:T(8,128)(2,1)S(1)}, u32[]{:S(2)}, u32[]{:S(2)}) collective-permute-start(bf16[1040,128]{1,0:T(8,128)(2,1)S(1)} %get-tuple-element.49), channel_id=1, source_target_pairs={{0,8},{8,0},{16,24},{24,16},{1,9},{9,1},{17,25},{25,17},{2,10},{10... | collective-permute-start | bytes 798728 | tf_op jit(solution)/shard_map/ppermute | solution.py:219
  61.8 3.5 %third_level.3 = (bf16[1040,128]{1,0:T(8,128)(2,1)S(1)}, bf16[1040,128]{1,0:T(8,128)(2,1)S(1)}, bf16[1040,128]{1,0:T(8,128)(2,1)S(1)}, bf16[1040,128]{1,0:T(8,128)(2,1)S(1)}) custom-call(s32[1,16]{1,0:T(1,128)} %bitcast.10, s32[4,64]{1,0:T(4,128)} %bitcast.8, bf16[8,256,256]{2,1,0:T(8,128)(2,1)S(1)} %copy-done.1, ...), custom_call_target="tpu_custom_call" | custom-call | flops 1073741824 | bytes 2097152 | tf_op jit(solution)/shard_map/third_level/pallas_call | solution.py:305
  65.3 3.3 %collective-permute-start.22 = (bf16[1040,128]{1,0:T(8,128)(2,1)S(1)}, bf16[1040,128]{1,0:T(8,128)(2,1)S(1)}, u32[]{:S(2)}, u32[]{:S(2)}) collective-permute-start(bf16[1040,128]{1,0:T(8,128)(2,1)S(1)} %get-tuple-element.61), channel_id=1, source_target_pairs={{0,16},{8,24},{16,0},{24,8},{1,17},{9,25},{17,1},{25,9},{2,18},{10... | collective-permute-start | bytes 798728 | tf_op jit(solution)/shard_map/ppermute | solution.py:219
  70.1 3.2 %collective-permute-done.12.refs_2_ = bf16[1040,128]{1,0:T(8,128)(2,1)S(1)} collective-permute-done((bf16[1040,128]{1,0:T(8,128)(2,1)S(1)}, bf16[1040,128]{1,0:T(8,128)(2,1)S(1)}, u32[]{:S(2)}, u32[]{:S(2)}) %collective-permute-start.12) | collective-permute-done | bytes 266272 | tf_op jit(solution)/shard_map/ppermute | solution.py:219
  73.3 4.6 %collective-permute-done.22.refs_4_ = bf16[1040,128]{1,0:T(8,128)(2,1)S(1)} collective-permute-done((bf16[1040,128]{1,0:T(8,128)(2,1)S(1)}, bf16[1040,128]{1,0:T(8,128)(2,1)S(1)}, u32[]{:S(2)}, u32[]{:S(2)}) %collective-permute-start.22) | collective-permute-done | bytes 266272 | tf_op jit(solution)/shard_map/ppermute | solution.py:219
  77.9 1.8 %collective-permute-done.23.refs_5_ = bf16[1040,128]{1,0:T(8,128)(2,1)S(1)} collective-permute-done((bf16[1040,128]{1,0:T(8,128)(2,1)S(1)}, bf16[1040,128]{1,0:T(8,128)(2,1)S(1)}, u32[]{:S(2)}, u32[]{:S(2)}) %collective-permute-start.23) | collective-permute-done | bytes 266272 | tf_op jit(solution)/shard_map/ppermute | solution.py:219
  79.6 3.2 %collective-permute-done.24.refs_6_ = bf16[1040,128]{1,0:T(8,128)(2,1)S(1)} collective-permute-done((bf16[1040,128]{1,0:T(8,128)(2,1)S(1)}, bf16[1040,128]{1,0:T(8,128)(2,1)S(1)}, u32[]{:S(2)}, u32[]{:S(2)}) %collective-permute-start.24) | collective-permute-done | bytes 266272 | tf_op jit(solution)/shard_map/ppermute | solution.py:219
  (36 shorter events, 9.0 us)
Async XLA Ops:
  4.9 6.2 %collective-permute-start = (bf16[8,32,128]{2,1,0:T(8,128)(2,1)S(1)}, bf16[8,32,128]{2,1,0:T(8,128)(2,1)S(1)}, u32[]{:S(2)}, u32[]{:S(2)}) collective-permute-start(bf16[8,32,128]{2,1,0:T(8,128)(2,1)S(1)} %get-tuple-element.35), channel_id=1, source_target_pairs={{0,4},{1,5},{2,6},{3,7},{4,0},{5,1},{6,2},{7,3},{8,12},{9,13},{10,... | collective-permute-start | bytes 196616 | tf_op jit(solution)/shard_map/ppermute | solution.py:219
  7.6 8.6 %collective-permute-start.1 = (bf16[8,32,128]{2,1,0:T(8,128)(2,1)S(1)}, bf16[8,32,128]{2,1,0:T(8,128)(2,1)S(1)}, u32[]{:S(2)}, u32[]{:S(2)}) collective-permute-start(bf16[8,32,128]{2,1,0:T(8,128)(2,1)S(1)} %get-tuple-element.36), channel_id=1, source_target_pairs={{0,5},{1,4},{2,7},{3,6},{4,1},{5,0},{6,3},{7,2},{8,13},{9,12},{10,... | collective-permute-start | bytes 196616 | tf_op jit(solution)/shard_map/ppermute | solution.py:219
  7.7 14.0 %collective-permute-start.6 = (bf16[16,32,128]{2,1,0:T(8,128)(2,1)S(1)}, bf16[16,32,128]{2,1,0:T(8,128)(2,1)S(1)}, u32[]{:S(2)}, u32[]{:S(2)}) collective-permute-start(bf16[16,32,128]{2,1,0:T(8,128)(2,1)S(1)} %get-tuple-element.41), channel_id=1, source_target_pairs={{0,1},{1,0},{2,3},{3,2},{4,5},{5,4},{6,7},{7,6},{8,9},{9,8},{10,11... | collective-permute-start | bytes 393224 | tf_op jit(solution)/shard_map/ppermute | solution.py:219
  8.0 8.8 %collective-permute-start.2 = (bf16[8,32,128]{2,1,0:T(8,128)(2,1)S(1)}, bf16[8,32,128]{2,1,0:T(8,128)(2,1)S(1)}, u32[]{:S(2)}, u32[]{:S(2)}) collective-permute-start(bf16[8,32,128]{2,1,0:T(8,128)(2,1)S(1)} %get-tuple-element.37), channel_id=1, source_target_pairs={{0,2},{1,3},{2,0},{3,1},{4,6},{5,7},{6,4},{7,5},{8,10},{9,11},{10,... | collective-permute-start | bytes 196616 | tf_op jit(solution)/shard_map/ppermute | solution.py:219
  11.0 5.8 %collective-permute-start.3 = (bf16[8,32,128]{2,1,0:T(8,128)(2,1)S(1)}, bf16[8,32,128]{2,1,0:T(8,128)(2,1)S(1)}, u32[]{:S(2)}, u32[]{:S(2)}) collective-permute-start(bf16[8,32,128]{2,1,0:T(8,128)(2,1)S(1)} %get-tuple-element.38), channel_id=1, source_target_pairs={{0,3},{1,2},{2,1},{3,0},{4,7},{5,6},{6,5},{7,4},{8,11},{9,10},{10,... | collective-permute-start | bytes 196616 | tf_op jit(solution)/shard_map/ppermute | solution.py:219
  11.1 7.5 %collective-permute-start.4 = (bf16[8,32,128]{2,1,0:T(8,128)(2,1)S(1)}, bf16[8,32,128]{2,1,0:T(8,128)(2,1)S(1)}, u32[]{:S(2)}, u32[]{:S(2)}) collective-permute-start(bf16[8,32,128]{2,1,0:T(8,128)(2,1)S(1)} %get-tuple-element.39), channel_id=1, source_target_pairs={{0,6},{1,7},{2,4},{3,5},{4,2},{5,3},{6,0},{7,1},{8,14},{9,15},{10,... | collective-permute-start | bytes 196616 | tf_op jit(solution)/shard_map/ppermute | solution.py:219
  23.6 13.4 %collective-permute-start.7 = (bf16[8,64,128]{2,1,0:T(8,128)(2,1)S(1)}, bf16[8,64,128]{2,1,0:T(8,128)(2,1)S(1)}, u32[]{:S(2)}, u32[]{:S(2)}) collective-permute-start(bf16[8,64,128]{2,1,0:T(8,128)(2,1)S(1)} %get-tuple-element.43), channel_id=1, source_target_pairs={{0,16},{8,24},{16,0},{24,8},{1,17},{9,25},{17,1},{25,9},{2,18},{10... | collective-permute-start | bytes 393224 | tf_op jit(solution)/shard_map/ppermute | solution.py:219
  28.3 8.8 %collective-permute-start.8 = (bf16[8,64,128]{2,1,0:T(8,128)(2,1)S(1)}, bf16[8,64,128]{2,1,0:T(8,128)(2,1)S(1)}, u32[]{:S(2)}, u32[]{:S(2)}) collective-permute-start(bf16[8,64,128]{2,1,0:T(8,128)(2,1)S(1)} %get-tuple-element.44), channel_id=1, source_target_pairs={{0,24},{8,16},{16,8},{24,0},{1,25},{9,17},{17,9},{25,1},{2,26},{10... | collective-permute-start | bytes 393224 | tf_op jit(solution)/shard_map/ppermute | solution.py:219
  29.3 9.6 %collective-permute-start.9 = (bf16[8,64,128]{2,1,0:T(8,128)(2,1)S(1)}, bf16[8,64,128]{2,1,0:T(8,128)(2,1)S(1)}, u32[]{:S(2)}, u32[]{:S(2)}) collective-permute-start(bf16[8,64,128]{2,1,0:T(8,128)(2,1)S(1)} %get-tuple-element.45), channel_id=1, source_target_pairs={{0,8},{8,0},{16,24},{24,16},{1,9},{9,1},{17,25},{25,17},{2,10},{10... | collective-permute-start | bytes 393224 | tf_op jit(solution)/shard_map/ppermute | solution.py:219
  29.8 7.2 %collective-permute-start.13 = (bf16[8,32,128]{2,1,0:T(8,128)(2,1)S(1)}, bf16[8,32,128]{2,1,0:T(8,128)(2,1)S(1)}, u32[]{:S(2)}, u32[]{:S(2)}) collective-permute-start(bf16[8,32,128]{2,1,0:T(8,128)(2,1)S(1)} %get-tuple-element.51), channel_id=1, source_target_pairs={{0,4},{1,5},{2,6},{3,7},{4,0},{5,1},{6,2},{7,3},{8,12},{9,13},{10,... | collective-permute-start | bytes 196616 | tf_op jit(solution)/shard_map/ppermute | solution.py:219
  29.8 16.0 %collective-permute-start.14 = (bf16[8,32,128]{2,1,0:T(8,128)(2,1)S(1)}, bf16[8,32,128]{2,1,0:T(8,128)(2,1)S(1)}, u32[]{:S(2)}, u32[]{:S(2)}) collective-permute-start(bf16[8,32,128]{2,1,0:T(8,128)(2,1)S(1)} %get-tuple-element.52), channel_id=1, source_target_pairs={{0,5},{1,4},{2,7},{3,6},{4,1},{5,0},{6,3},{7,2},{8,13},{9,12},{10,... | collective-permute-start | bytes 196616 | tf_op jit(solution)/shard_map/ppermute | solution.py:219
  37.0 11.2 %collective-permute-start.15 = (bf16[8,32,128]{2,1,0:T(8,128)(2,1)S(1)}, bf16[8,32,128]{2,1,0:T(8,128)(2,1)S(1)}, u32[]{:S(2)}, u32[]{:S(2)}) collective-permute-start(bf16[8,32,128]{2,1,0:T(8,128)(2,1)S(1)} %get-tuple-element.53), channel_id=1, source_target_pairs={{0,2},{1,3},{2,0},{3,1},{4,6},{5,7},{6,4},{7,5},{8,10},{9,11},{10,... | collective-permute-start | bytes 196616 | tf_op jit(solution)/shard_map/ppermute | solution.py:219
  37.0 11.2 %collective-permute-start.16 = (bf16[8,32,128]{2,1,0:T(8,128)(2,1)S(1)}, bf16[8,32,128]{2,1,0:T(8,128)(2,1)S(1)}, u32[]{:S(2)}, u32[]{:S(2)}) collective-permute-start(bf16[8,32,128]{2,1,0:T(8,128)(2,1)S(1)} %get-tuple-element.54), channel_id=1, source_target_pairs={{0,3},{1,2},{2,1},{3,0},{4,7},{5,6},{6,5},{7,4},{8,11},{9,10},{10,... | collective-permute-start | bytes 196616 | tf_op jit(solution)/shard_map/ppermute | solution.py:219
  37.0 11.2 %collective-permute-start.17 = (bf16[8,32,128]{2,1,0:T(8,128)(2,1)S(1)}, bf16[8,32,128]{2,1,0:T(8,128)(2,1)S(1)}, u32[]{:S(2)}, u32[]{:S(2)}) collective-permute-start(bf16[8,32,128]{2,1,0:T(8,128)(2,1)S(1)} %get-tuple-element.55), channel_id=1, source_target_pairs={{0,6},{1,7},{2,4},{3,5},{4,2},{5,3},{6,0},{7,1},{8,14},{9,15},{10,... | collective-permute-start | bytes 196616 | tf_op jit(solution)/shard_map/ppermute | solution.py:219
  38.9 9.3 %collective-permute-start.18 = (bf16[8,32,128]{2,1,0:T(8,128)(2,1)S(1)}, bf16[8,32,128]{2,1,0:T(8,128)(2,1)S(1)}, u32[]{:S(2)}, u32[]{:S(2)}) collective-permute-start(bf16[8,32,128]{2,1,0:T(8,128)(2,1)S(1)} %get-tuple-element.56), channel_id=1, source_target_pairs={{0,7},{1,6},{2,5},{3,4},{4,3},{5,2},{6,1},{7,0},{8,15},{9,14},{10,... | collective-permute-start | bytes 196616 | tf_op jit(solution)/shard_map/ppermute | solution.py:219
  45.8 24.3 %collective-permute-start.10 = (bf16[1040,128]{1,0:T(8,128)(2,1)S(1)}, bf16[1040,128]{1,0:T(8,128)(2,1)S(1)}, u32[]{:S(2)}, u32[]{:S(2)}) collective-permute-start(bf16[1040,128]{1,0:T(8,128)(2,1)S(1)} %get-tuple-element.47), channel_id=1, source_target_pairs={{0,16},{8,24},{16,0},{24,8},{1,17},{9,25},{17,1},{25,9},{2,18},{10... | collective-permute-start | bytes 798728 | tf_op jit(solution)/shard_map/ppermute | solution.py:219
  50.0 8.2 %collective-permute-start.19 = (bf16[8,64,128]{2,1,0:T(8,128)(2,1)S(1)}, bf16[8,64,128]{2,1,0:T(8,128)(2,1)S(1)}, u32[]{:S(2)}, u32[]{:S(2)}) collective-permute-start(bf16[8,64,128]{2,1,0:T(8,128)(2,1)S(1)} %get-tuple-element.57), channel_id=1, source_target_pairs={{0,16},{8,24},{16,0},{24,8},{1,17},{9,25},{17,1},{25,9},{2,18},{10... | collective-permute-start | bytes 393224 | tf_op jit(solution)/shard_map/ppermute | solution.py:219
  52.4 9.3 %collective-permute-start.20 = (bf16[8,64,128]{2,1,0:T(8,128)(2,1)S(1)}, bf16[8,64,128]{2,1,0:T(8,128)(2,1)S(1)}, u32[]{:S(2)}, u32[]{:S(2)}) collective-permute-start(bf16[8,64,128]{2,1,0:T(8,128)(2,1)S(1)} %get-tuple-element.58), channel_id=1, source_target_pairs={{0,24},{8,16},{16,8},{24,0},{1,25},{9,17},{17,9},{25,1},{2,26},{10... | collective-permute-start | bytes 393224 | tf_op jit(solution)/shard_map/ppermute | solution.py:219
  55.1 6.7 %collective-permute-start.21 = (bf16[8,64,128]{2,1,0:T(8,128)(2,1)S(1)}, bf16[8,64,128]{2,1,0:T(8,128)(2,1)S(1)}, u32[]{:S(2)}, u32[]{:S(2)}) collective-permute-start(bf16[8,64,128]{2,1,0:T(8,128)(2,1)S(1)} %get-tuple-element.59), channel_id=1, source_target_pairs={{0,8},{8,0},{16,24},{24,16},{1,9},{9,1},{17,25},{25,17},{2,10},{10... | collective-permute-start | bytes 393224 | tf_op jit(solution)/shard_map/ppermute | solution.py:219
  55.1 15.0 %collective-permute-start.11 = (bf16[1040,128]{1,0:T(8,128)(2,1)S(1)}, bf16[1040,128]{1,0:T(8,128)(2,1)S(1)}, u32[]{:S(2)}, u32[]{:S(2)}) collective-permute-start(bf16[1040,128]{1,0:T(8,128)(2,1)S(1)} %get-tuple-element.48), channel_id=1, source_target_pairs={{0,24},{8,16},{16,8},{24,0},{1,25},{9,17},{17,9},{25,1},{2,26},{10... | collective-permute-start | bytes 798728 | tf_op jit(solution)/shard_map/ppermute | solution.py:219
  58.2 15.0 %collective-permute-start.12 = (bf16[1040,128]{1,0:T(8,128)(2,1)S(1)}, bf16[1040,128]{1,0:T(8,128)(2,1)S(1)}, u32[]{:S(2)}, u32[]{:S(2)}) collective-permute-start(bf16[1040,128]{1,0:T(8,128)(2,1)S(1)} %get-tuple-element.49), channel_id=1, source_target_pairs={{0,8},{8,0},{16,24},{24,16},{1,9},{9,1},{17,25},{25,17},{2,10},{10... | collective-permute-start | bytes 798728 | tf_op jit(solution)/shard_map/ppermute | solution.py:219
  65.3 12.6 %collective-permute-start.22 = (bf16[1040,128]{1,0:T(8,128)(2,1)S(1)}, bf16[1040,128]{1,0:T(8,128)(2,1)S(1)}, u32[]{:S(2)}, u32[]{:S(2)}) collective-permute-start(bf16[1040,128]{1,0:T(8,128)(2,1)S(1)} %get-tuple-element.61), channel_id=1, source_target_pairs={{0,16},{8,24},{16,0},{24,8},{1,17},{9,25},{17,1},{25,9},{2,18},{10... | collective-permute-start | bytes 798728 | tf_op jit(solution)/shard_map/ppermute | solution.py:219
  68.6 11.1 %collective-permute-start.23 = (bf16[1040,128]{1,0:T(8,128)(2,1)S(1)}, bf16[1040,128]{1,0:T(8,128)(2,1)S(1)}, u32[]{:S(2)}, u32[]{:S(2)}) collective-permute-start(bf16[1040,128]{1,0:T(8,128)(2,1)S(1)} %get-tuple-element.62), channel_id=1, source_target_pairs={{0,24},{8,16},{16,8},{24,0},{1,25},{9,17},{17,9},{25,1},{2,26},{10... | collective-permute-start | bytes 798728 | tf_op jit(solution)/shard_map/ppermute | solution.py:219
  70.0 12.8 %collective-permute-start.24 = (bf16[1040,128]{1,0:T(8,128)(2,1)S(1)}, bf16[1040,128]{1,0:T(8,128)(2,1)S(1)}, u32[]{:S(2)}, u32[]{:S(2)}) collective-permute-start(bf16[1040,128]{1,0:T(8,128)(2,1)S(1)} %get-tuple-element.63), channel_id=1, source_target_pairs={{0,8},{8,0},{16,24},{24,16},{1,9},{9,1},{17,25},{25,17},{2,10},{10... | collective-permute-start | bytes 798728 | tf_op jit(solution)/shard_map/ppermute | solution.py:219
  (3 other events, 47.8 us)
where the time goes:
time: 84.6 us; the launch traced here: 84.4 us
  starting transfers between devices  42.7 us (50%)
  waiting for transfers between devices  24.5 us (29%)
  Pallas kernels  17 us (20%)
    ppermute x25, starting transfers between devices, exchange(): lax.ppermute(part, axis, [(i, i ^ r) for i in range(size)])  42.7 us
    ppermute x25, waiting for transfers between devices, exchange(): lax.ppermute(part, axis, [(i, i ^ r) for i in range(size)])  24.5 us
    pallas_call x2, Pallas kernels, per_device(): third(owners, pairs_third, matrices_third, *parts)  6.9 us
    pallas_call x1, Pallas kernels, per_device(): pl.pallas_call(functools.partial(first_kernel, narrow), out_shape=blocks(...  4.88 us
    pallas_call x2, Pallas kernels, per_device(): second(chunk)(pairs_second, matrices_second, *parts, *near)  3.72 us
  transfers between devices with their start and end apart: 25, of which 9 were waited for; matrix products, arithmetic and copies ran while one was open for 0% of the time, Pallas kernels for 10%

commit v1 on v0

--- a/solution.py
+++ b/solution.py
@@ -189,28 +189,47 @@
         ).astype(jnp.bfloat16)
 
 
-def last_kernel(wide, *refs):
-    ins, out, flags = refs[: 2 * wide], refs[2 * wide], refs[2 * wide + 1]
+def place_kernel(wide, chosen, *refs):
+    count = len(chosen)
+    firsts, seconds = refs[:wide], refs[wide : wide + count]
+    out, stage, flags, sems = refs[-4:]
     boxes, width, columns = out.shape
     room = 2 * boxes // wide
     me = lax.axis_index("wide")
-    for at, r in enumerate(steps(wide)):
-        mark = ins[at][pl.ds(room // 2 * width, 16), :].astype(jnp.float32)
+    order = steps(wide)
+    for at, r in enumerate(order):
+        mark = firsts[at][pl.ds(room // 2 * width, 16), :].astype(jnp.float32)
         flags[me ^ r] = (jnp.max(mark) > 0.5).astype(jnp.int32)
     left = left_half((width, columns))
-    for at, r in enumerate(steps(wide)):
+    moves = []
+    for at, r in enumerate(chosen):
         origin = me ^ r
         base = jnp.int32(0)
         for w in range(wide):
             base = base + jnp.where(w < origin, flags[w], 0) * room
+        copies = [
+            pltpu.make_async_copy(
+                stage.at[pl.ds(base + 2 * p, 2)], out.at[pl.ds(base + 2 * p, 2)], sems.at[at, p]
+            )
+            for p in range(room // 2)
+        ]
+        moves.append((origin, copies))
 
         @pl.when(flags[origin] > 0)
-        def _(at=at, base=base):
-            for p in range(room // 2):
-                a = ins[at][pl.ds(p * width, width), :]
-                b = ins[wide + at][pl.ds(p * width, width), :]
-                out[base + 2 * p] = jnp.where(left, a, swap(b))
-                out[base + 2 * p + 1] = jnp.where(left, swap(a), b)
+        def _(a_ref=firsts[order.index(r)], b_ref=seconds[at], base=base, copies=copies):
+            for p, copy in enumerate(copies):
+                a = a_ref[pl.ds(p * width, width), :]
+                b = b_ref[pl.ds(p * width, width), :]
+                stage[base + 2 * p] = jnp.where(left, a, swap(b))
+                stage[base + 2 * p + 1] = jnp.where(left, swap(a), b)
+                copy.start()
+
+    for origin, copies in moves:
+
+        @pl.when(flags[origin] > 0)
+        def _(copies=copies):
+            for copy in copies:
+                copy.wait()
 
 
 def exchange(parts, axis, size, order):
@@ -307,15 +326,27 @@
         )
         for parts in moved
     ]
-    return pl.pallas_call(
-        functools.partial(last_kernel, wide),
-        out_shape=jax.ShapeDtypeStruct((boxes, width, columns), jnp.bfloat16),
-        in_specs=[VMEM] * (2 * wide),
-        out_specs=VMEM,
-        scratch_shapes=[pltpu.SMEM((wide,), jnp.int32)],
-        compiler_params=GRANT,
-        name="place",
-    )(*moved[0], *moved[1])
+    firsts, seconds = moved
+    late = steps(wide).index(1)
+    early = [r for r in steps(wide) if r != 1]
+
+    def place(chosen, parts, start=()):
+        return pl.pallas_call(
+            functools.partial(place_kernel, wide, chosen),
+            out_shape=jax.ShapeDtypeStruct((boxes, width, columns), jnp.bfloat16),
+            in_specs=[VMEM] * (wide + len(parts)) + [HBM] * len(start),
+            out_specs=HBM,
+            input_output_aliases={wide + len(parts): 0} if start else {},
+            scratch_shapes=[
+                pltpu.VMEM((boxes, width, columns), jnp.bfloat16),
+                pltpu.SMEM((wide,), jnp.int32),
+                pltpu.SemaphoreType.DMA((len(chosen), room // 2)),
+            ],
+            compiler_params=GRANT,
+        )(*firsts, *parts, *start)
+
+    begun = place(early, seconds[:late] + seconds[late + 1 :])
+    return place([1], [seconds[late]], [begun])
 
 
 def solution(mesh):

time: 84.6 us -> 84.1 us (level)
  waiting for transfers between devices: 24.5 us -> 23.4 us
    ppermute x25, waiting for transfers between devices: 24.5 us -> 23.4 us  [exchange(): lax.ppermute(part, axis, [(i, i ^ r) for i in range(size)])]
    pallas_call x1 -> x2, Pallas kernels: 1.53 us -> 2.18 us  [place(): pl.pallas_call(functools.partial(place_kernel, wide, chosen), out_shape=j...]
  transfers between devices with their start and end apart: 25 -> 25, of which waited for: 9 -> 9; matrix products, arithmetic and copies ran while one was open for 0% -> 0% of each run, Pallas kernels for 10% -> 12%
where the time goes in v1:
time: 84.1 us; the launch traced here: 83.9 us
  starting transfers between devices  42.7 us (51%)
  waiting for transfers between devices  23.4 us (28%)
  Pallas kernels  17.7 us (21%)
    ppermute x25, starting transfers between devices, exchange(): lax.ppermute(part, axis, [(i, i ^ r) for i in range(size)])  42.7 us
    ppermute x25, waiting for transfers between devices, exchange(): lax.ppermute(part, axis, [(i, i ^ r) for i in range(size)])  23.4 us
    pallas_call x2, Pallas kernels, per_device(): third(owners, pairs_third, matrices_third, *parts)  6.89 us
    pallas_call x1, Pallas kernels, per_device(): pl.pallas_call(functools.partial(first_kernel, narrow), out_shape=blocks(...  4.88 us
    pallas_call x2, Pallas kernels, per_device(): second(chunk)(pairs_second, matrices_second, *parts, *near)  3.72 us
    pallas_call x2, Pallas kernels, place(): pl.pallas_call(functools.partial(place_kernel, wide, chosen), out_shape=j...  2.18 us
  transfers between devices with their start and end apart: 25, of which 9 were waited for; matrix products, arithmetic and copies ran while one was open for 0% of the time, Pallas kernels for 12%

profile of v1, /device:TPU:0, one launch (start us, length us, event | category | flops | bytes accessed | tf_op | source)
XLA Modules:
  0.0 83.9 jit_solution(15375335864513671263)
XLA Ops:
  0.0 4.9 %first_level.1 = (bf16[8,32,128]{2,1,0:T(8,128)(2,1)S(1)}, bf16[8,32,128]{2,1,0:T(8,128)(2,1)S(1)}, bf16[8,32,128]{2,1,0:T(8,128)(2,1)S(1)}, bf16[8,32,128]{2,1,...) custom-call(s32[4,64]{1,0:T(4,128)} %bitcast.4, ...), custom_call_target="tpu_custom_call" | custom-call | flops 1073741824 | bytes 2097152 | tf_op jit(solution)/shard_map/first_level/pallas_call | solution.py:267
  4.9 2.7 %collective-permute-start = (bf16[8,32,128]{2,1,0:T(8,128)(2,1)S(1)}, bf16[8,32,128]{2,1,0:T(8,128)(2,1)S(1)}, u32[]{:S(2)}, u32[]{:S(2)}) collective-permute-start(bf16[8,32,128]{2,1,0:T(8,128)(2,1)S(1)} %get-tuple-element.35), channel_id=1, source_target_pairs={{0,4},{1,5},{2,6},{3,7},{4,0},{5,1},{6,2},{7,3},{8,12},{9,13},{10,... | collective-permute-start | bytes 196616 | tf_op jit(solution)/shard_map/ppermute | solution.py:238
  8.0 3.1 %collective-permute-start.2 = (bf16[8,32,128]{2,1,0:T(8,128)(2,1)S(1)}, bf16[8,32,128]{2,1,0:T(8,128)(2,1)S(1)}, u32[]{:S(2)}, u32[]{:S(2)}) collective-permute-start(bf16[8,32,128]{2,1,0:T(8,128)(2,1)S(1)} %get-tuple-element.37), channel_id=1, source_target_pairs={{0,2},{1,3},{2,0},{3,1},{4,6},{5,7},{6,4},{7,5},{8,10},{9,11},{10,... | collective-permute-start | bytes 196616 | tf_op jit(solution)/shard_map/ppermute | solution.py:238
  11.1 5.2 %collective-permute-start.4 = (bf16[8,32,128]{2,1,0:T(8,128)(2,1)S(1)}, bf16[8,32,128]{2,1,0:T(8,128)(2,1)S(1)}, u32[]{:S(2)}, u32[]{:S(2)}) collective-permute-start(bf16[8,32,128]{2,1,0:T(8,128)(2,1)S(1)} %get-tuple-element.39), channel_id=1, source_target_pairs={{0,6},{1,7},{2,4},{3,5},{4,2},{5,3},{6,0},{7,1},{8,14},{9,15},{10,... | collective-permute-start | bytes 196616 | tf_op jit(solution)/shard_map/ppermute | solution.py:238
  16.8 1.7 %collective-permute-done.4.refs_4_ = bf16[8,32,128]{2,1,0:T(8,128)(2,1)S(1)} collective-permute-done((bf16[8,32,128]{2,1,0:T(8,128)(2,1)S(1)}, bf16[8,32,128]{2,1,0:T(8,128)(2,1)S(1)}, u32[]{:S(2)}, u32[]{:S(2)}) %collective-permute-start.4) | collective-permute-done | bytes 65568 | tf_op jit(solution)/shard_map/ppermute | solution.py:238
  18.6 3.1 %collective-permute-done.5.refs_5_ = bf16[8,32,128]{2,1,0:T(8,128)(2,1)S(1)} collective-permute-done((bf16[8,32,128]{2,1,0:T(8,128)(2,1)S(1)}, bf16[8,32,128]{2,1,0:T(8,128)(2,1)S(1)}, u32[]{:S(2)}, u32[]{:S(2)}) %collective-permute-start.5) | collective-permute-done | bytes 65568 | tf_op jit(solution)/shard_map/ppermute | solution.py:238
  21.7 1.9 %second_level.2 = (bf16[8,64,128]{2,1,0:T(8,128)(2,1)S(1)}, bf16[8,64,128]{2,1,0:T(8,128)(2,1)S(1)}, bf16[8,64,128]{2,1,0:T(8,128)(2,1)S(1)}, bf16[8,64,128]{2,1,0:T(8,128)(2,1)S(1)}) custom-call(s32[4,64]{1,0:T(4,128)} %bitcast.5, bf16[8,256,256]{2,1,0:T(8,128)(2,1)S(1)} %copy-done, bf16[8,32,128]{2,1,0:T(8,128)(2,1)S(1)} %collective-permute-done.refs_0_, ...), custom_call_target="tpu_custom_call" | custom-call | flops 1073741824 | bytes 2097152 | tf_op jit(solution)/shard_map/second_level/pallas_call | solution.py:317
  23.6 4.6 %collective-permute-start.7 = (bf16[8,64,128]{2,1,0:T(8,128)(2,1)S(1)}, bf16[8,64,128]{2,1,0:T(8,128)(2,1)S(1)}, u32[]{:S(2)}, u32[]{:S(2)}) collective-permute-start(bf16[8,64,128]{2,1,0:T(8,128)(2,1)S(1)} %get-tuple-element.43), channel_id=1, source_target_pairs={{0,16},{8,24},{16,0},{24,8},{1,17},{9,25},{17,1},{25,9},{2,18},{10... | collective-permute-start | bytes 393224 | tf_op jit(solution)/shard_map/ppermute | solution.py:238
  29.8 2.1 %collective-permute-start.14 = (bf16[8,32,128]{2,1,0:T(8,128)(2,1)S(1)}, bf16[8,32,128]{2,1,0:T(8,128)(2,1)S(1)}, u32[]{:S(2)}, u32[]{:S(2)}) collective-permute-start(bf16[8,32,128]{2,1,0:T(8,128)(2,1)S(1)} %get-tuple-element.52), channel_id=1, source_target_pairs={{0,5},{1,4},{2,7},{3,6},{4,1},{5,0},{6,3},{7,2},{8,13},{9,12},{10,... | collective-permute-start | bytes 196616 | tf_op jit(solution)/shard_map/ppermute | solution.py:238
  31.9 5.1 %collective-permute-done.13.refs_0_ = bf16[8,32,128]{2,1,0:T(8,128)(2,1)S(1)} collective-permute-done((bf16[8,32,128]{2,1,0:T(8,128)(2,1)S(1)}, bf16[8,32,128]{2,1,0:T(8,128)(2,1)S(1)}, u32[]{:S(2)}, u32[]{:S(2)}) %collective-permute-start.13) | collective-permute-done | bytes 65568 | tf_op jit(solution)/shard_map/ppermute | solution.py:238
  37.0 1.8 %collective-permute-start.17 = (bf16[8,32,128]{2,1,0:T(8,128)(2,1)S(1)}, bf16[8,32,128]{2,1,0:T(8,128)(2,1)S(1)}, u32[]{:S(2)}, u32[]{:S(2)}) collective-permute-start(bf16[8,32,128]{2,1,0:T(8,128)(2,1)S(1)} %get-tuple-element.55), channel_id=1, source_target_pairs={{0,6},{1,7},{2,4},{3,5},{4,2},{5,3},{6,0},{7,1},{8,14},{9,15},{10,... | collective-permute-start | bytes 196616 | tf_op jit(solution)/shard_map/ppermute | solution.py:238
  38.9 3.4 %collective-permute-start.18 = (bf16[8,32,128]{2,1,0:T(8,128)(2,1)S(1)}, bf16[8,32,128]{2,1,0:T(8,128)(2,1)S(1)}, u32[]{:S(2)}, u32[]{:S(2)}) collective-permute-start(bf16[8,32,128]{2,1,0:T(8,128)(2,1)S(1)} %get-tuple-element.56), channel_id=1, source_target_pairs={{0,7},{1,6},{2,5},{3,4},{4,3},{5,2},{6,1},{7,0},{8,15},{9,14},{10,... | collective-permute-start | bytes 196616 | tf_op jit(solution)/shard_map/ppermute | solution.py:238
  42.3 3.4 %third_level.2 = (bf16[1040,128]{1,0:T(8,128)(2,1)S(1)}, bf16[1040,128]{1,0:T(8,128)(2,1)S(1)}, bf16[1040,128]{1,0:T(8,128)(2,1)S(1)}, bf16[1040,128]{1,0:T(8,128)(2,1)S(1)}) custom-call(s32[1,16]{1,0:T(1,128)} %bitcast.9, s32[4,64]{1,0:T(4,128)} %bitcast.7, bf16[8,256,256]{2,1,0:T(8,128)(2,1)S(1)} %copy-done.1, ...), custom_call_target="tpu_custom_call" | custom-call | flops 1073741824 | bytes 2097152 | tf_op jit(solution)/shard_map/third_level/pallas_call | solution.py:324
  45.8 2.4 %collective-permute-start.10 = (bf16[1040,128]{1,0:T(8,128)(2,1)S(1)}, bf16[1040,128]{1,0:T(8,128)(2,1)S(1)}, u32[]{:S(2)}, u32[]{:S(2)}) collective-permute-start(bf16[1040,128]{1,0:T(8,128)(2,1)S(1)} %get-tuple-element.47), channel_id=1, source_target_pairs={{0,16},{8,24},{16,0},{24,8},{1,17},{9,25},{17,1},{25,9},{2,18},{10... | collective-permute-start | bytes 798728 | tf_op jit(solution)/shard_map/ppermute | solution.py:238
  48.2 1.8 %second_level.3 = (bf16[8,64,128]{2,1,0:T(8,128)(2,1)S(1)}, bf16[8,64,128]{2,1,0:T(8,128)(2,1)S(1)}, bf16[8,64,128]{2,1,0:T(8,128)(2,1)S(1)}, bf16[8,64,128]{2,1,0:T(8,128)(2,1)S(1)}) custom-call(s32[4,64]{1,0:T(4,128)} %bitcast.6, bf16[8,256,256]{2,1,0:T(8,128)(2,1)S(1)} %copy-done, bf16[8,32,128]{2,1,0:T(8,128)(2,1)S(1)} %collective-permute-done.13.refs_0_, ...), custom_call_target="tpu_custom_call" | custom-call | flops 1073741824 | bytes 2097152 | tf_op jit(solution)/shard_map/second_level/pallas_call | solution.py:317
  50.0 2.3 %collective-permute-start.19 = (bf16[8,64,128]{2,1,0:T(8,128)(2,1)S(1)}, bf16[8,64,128]{2,1,0:T(8,128)(2,1)S(1)}, u32[]{:S(2)}, u32[]{:S(2)}) collective-permute-start(bf16[8,64,128]{2,1,0:T(8,128)(2,1)S(1)} %get-tuple-element.57), channel_id=1, source_target_pairs={{0,16},{8,24},{16,0},{24,8},{1,17},{9,25},{17,1},{25,9},{2,18},{10... | collective-permute-start | bytes 393224 | tf_op jit(solution)/shard_map/ppermute | solution.py:238
  52.4 2.7 %collective-permute-start.20 = (bf16[8,64,128]{2,1,0:T(8,128)(2,1)S(1)}, bf16[8,64,128]{2,1,0:T(8,128)(2,1)S(1)}, u32[]{:S(2)}, u32[]{:S(2)}) collective-permute-start(bf16[8,64,128]{2,1,0:T(8,128)(2,1)S(1)} %get-tuple-element.58), channel_id=1, source_target_pairs={{0,24},{8,16},{16,8},{24,0},{1,25},{9,17},{17,9},{25,1},{2,26},{10... | collective-permute-start | bytes 393224 | tf_op jit(solution)/shard_map/ppermute | solution.py:238
  58.2 3.4 %collective-permute-start.12 = (bf16[1040,128]{1,0:T(8,128)(2,1)S(1)}, bf16[1040,128]{1,0:T(8,128)(2,1)S(1)}, u32[]{:S(2)}, u32[]{:S(2)}) collective-permute-start(bf16[1040,128]{1,0:T(8,128)(2,1)S(1)} %get-tuple-element.49), channel_id=1, source_target_pairs={{0,8},{8,0},{16,24},{24,16},{1,9},{9,1},{17,25},{25,17},{2,10},{10... | collective-permute-start | bytes 798728 | tf_op jit(solution)/shard_map/ppermute | solution.py:238
  61.8 3.4 %third_level.3 = (bf16[1040,128]{1,0:T(8,128)(2,1)S(1)}, bf16[1040,128]{1,0:T(8,128)(2,1)S(1)}, bf16[1040,128]{1,0:T(8,128)(2,1)S(1)}, bf16[1040,128]{1,0:T(8,128)(2,1)S(1)}) custom-call(s32[1,16]{1,0:T(1,128)} %bitcast.10, s32[4,64]{1,0:T(4,128)} %bitcast.8, bf16[8,256,256]{2,1,0:T(8,128)(2,1)S(1)} %copy-done.1, ...), custom_call_target="tpu_custom_call" | custom-call | flops 1073741824 | bytes 2097152 | tf_op jit(solution)/shard_map/third_level/pallas_call | solution.py:324
  65.3 3.3 %collective-permute-start.23 = (bf16[1040,128]{1,0:T(8,128)(2,1)S(1)}, bf16[1040,128]{1,0:T(8,128)(2,1)S(1)}, u32[]{:S(2)}, u32[]{:S(2)}) collective-permute-start(bf16[1040,128]{1,0:T(8,128)(2,1)S(1)} %get-tuple-element.62), channel_id=1, source_target_pairs={{0,16},{8,24},{16,0},{24,8},{1,17},{9,25},{17,1},{25,9},{2,18},{10... | collective-permute-start | bytes 798728 | tf_op jit(solution)/shard_map/ppermute | solution.py:238
  70.1 3.2 %collective-permute-done.12.refs_2_ = bf16[1040,128]{1,0:T(8,128)(2,1)S(1)} collective-permute-done((bf16[1040,128]{1,0:T(8,128)(2,1)S(1)}, bf16[1040,128]{1,0:T(8,128)(2,1)S(1)}, u32[]{:S(2)}, u32[]{:S(2)}) %collective-permute-start.12) | collective-permute-done | bytes 266272 | tf_op jit(solution)/shard_map/ppermute | solution.py:238
  73.3 4.6 %collective-permute-done.23.refs_4_ = bf16[1040,128]{1,0:T(8,128)(2,1)S(1)} collective-permute-done((bf16[1040,128]{1,0:T(8,128)(2,1)S(1)}, bf16[1040,128]{1,0:T(8,128)(2,1)S(1)}, u32[]{:S(2)}, u32[]{:S(2)}) %collective-permute-start.23) | collective-permute-done | bytes 266272 | tf_op jit(solution)/shard_map/ppermute | solution.py:238
  77.9 1.8 %collective-permute-done.24.refs_5_ = bf16[1040,128]{1,0:T(8,128)(2,1)S(1)} collective-permute-done((bf16[1040,128]{1,0:T(8,128)(2,1)S(1)}, bf16[1040,128]{1,0:T(8,128)(2,1)S(1)}, u32[]{:S(2)}, u32[]{:S(2)}) %collective-permute-start.24) | collective-permute-done | bytes 266272 | tf_op jit(solution)/shard_map/ppermute | solution.py:238
  80.8 2.1 %collective-permute-done.22.refs_4_ = bf16[1040,128]{1,0:T(8,128)(2,1)S(1)} collective-permute-done((bf16[1040,128]{1,0:T(8,128)(2,1)S(1)}, bf16[1040,128]{1,0:T(8,128)(2,1)S(1)}, u32[]{:S(2)}, u32[]{:S(2)}) %collective-permute-start.22) | collective-permute-done | bytes 266272 | tf_op jit(solution)/shard_map/ppermute | solution.py:238
  (37 shorter events, 9.6 us)
Async XLA Ops:
  4.9 6.2 %collective-permute-start = (bf16[8,32,128]{2,1,0:T(8,128)(2,1)S(1)}, bf16[8,32,128]{2,1,0:T(8,128)(2,1)S(1)}, u32[]{:S(2)}, u32[]{:S(2)}) collective-permute-start(bf16[8,32,128]{2,1,0:T(8,128)(2,1)S(1)} %get-tuple-element.35), channel_id=1, source_target_pairs={{0,4},{1,5},{2,6},{3,7},{4,0},{5,1},{6,2},{7,3},{8,12},{9,13},{10,... | collective-permute-start | bytes 196616 | tf_op jit(solution)/shard_map/ppermute | solution.py:238
  7.6 8.6 %collective-permute-start.1 = (bf16[8,32,128]{2,1,0:T(8,128)(2,1)S(1)}, bf16[8,32,128]{2,1,0:T(8,128)(2,1)S(1)}, u32[]{:S(2)}, u32[]{:S(2)}) collective-permute-start(bf16[8,32,128]{2,1,0:T(8,128)(2,1)S(1)} %get-tuple-element.36), channel_id=1, source_target_pairs={{0,5},{1,4},{2,7},{3,6},{4,1},{5,0},{6,3},{7,2},{8,13},{9,12},{10,... | collective-permute-start | bytes 196616 | tf_op jit(solution)/shard_map/ppermute | solution.py:238
  7.7 14.0 %collective-permute-start.6 = (bf16[16,32,128]{2,1,0:T(8,128)(2,1)S(1)}, bf16[16,32,128]{2,1,0:T(8,128)(2,1)S(1)}, u32[]{:S(2)}, u32[]{:S(2)}) collective-permute-start(bf16[16,32,128]{2,1,0:T(8,128)(2,1)S(1)} %get-tuple-element.41), channel_id=1, source_target_pairs={{0,1},{1,0},{2,3},{3,2},{4,5},{5,4},{6,7},{7,6},{8,9},{9,8},{10,11... | collective-permute-start | bytes 393224 | tf_op jit(solution)/shard_map/ppermute | solution.py:238
  8.0 8.8 %collective-permute-start.2 = (bf16[8,32,128]{2,1,0:T(8,128)(2,1)S(1)}, bf16[8,32,128]{2,1,0:T(8,128)(2,1)S(1)}, u32[]{:S(2)}, u32[]{:S(2)}) collective-permute-start(bf16[8,32,128]{2,1,0:T(8,128)(2,1)S(1)} %get-tuple-element.37), channel_id=1, source_target_pairs={{0,2},{1,3},{2,0},{3,1},{4,6},{5,7},{6,4},{7,5},{8,10},{9,11},{10,... | collective-permute-start | bytes 196616 | tf_op jit(solution)/shard_map/ppermute | solution.py:238
  11.0 5.8 %collective-permute-start.3 = (bf16[8,32,128]{2,1,0:T(8,128)(2,1)S(1)}, bf16[8,32,128]{2,1,0:T(8,128)(2,1)S(1)}, u32[]{:S(2)}, u32[]{:S(2)}) collective-permute-start(bf16[8,32,128]{2,1,0:T(8,128)(2,1)S(1)} %get-tuple-element.38), channel_id=1, source_target_pairs={{0,3},{1,2},{2,1},{3,0},{4,7},{5,6},{6,5},{7,4},{8,11},{9,10},{10,... | collective-permute-start | bytes 196616 | tf_op jit(solution)/shard_map/ppermute | solution.py:238
  11.1 7.5 %collective-permute-start.4 = (bf16[8,32,128]{2,1,0:T(8,128)(2,1)S(1)}, bf16[8,32,128]{2,1,0:T(8,128)(2,1)S(1)}, u32[]{:S(2)}, u32[]{:S(2)}) collective-permute-start(bf16[8,32,128]{2,1,0:T(8,128)(2,1)S(1)} %get-tuple-element.39), channel_id=1, source_target_pairs={{0,6},{1,7},{2,4},{3,5},{4,2},{5,3},{6,0},{7,1},{8,14},{9,15},{10,... | collective-permute-start | bytes 196616 | tf_op jit(solution)/shard_map/ppermute | solution.py:238
  23.6 13.4 %collective-permute-start.7 = (bf16[8,64,128]{2,1,0:T(8,128)(2,1)S(1)}, bf16[8,64,128]{2,1,0:T(8,128)(2,1)S(1)}, u32[]{:S(2)}, u32[]{:S(2)}) collective-permute-start(bf16[8,64,128]{2,1,0:T(8,128)(2,1)S(1)} %get-tuple-element.43), channel_id=1, source_target_pairs={{0,16},{8,24},{16,0},{24,8},{1,17},{9,25},{17,1},{25,9},{2,18},{10... | collective-permute-start | bytes 393224 | tf_op jit(solution)/shard_map/ppermute | solution.py:238
  28.3 8.8 %collective-permute-start.8 = (bf16[8,64,128]{2,1,0:T(8,128)(2,1)S(1)}, bf16[8,64,128]{2,1,0:T(8,128)(2,1)S(1)}, u32[]{:S(2)}, u32[]{:S(2)}) collective-permute-start(bf16[8,64,128]{2,1,0:T(8,128)(2,1)S(1)} %get-tuple-element.44), channel_id=1, source_target_pairs={{0,24},{8,16},{16,8},{24,0},{1,25},{9,17},{17,9},{25,1},{2,26},{10... | collective-permute-start | bytes 393224 | tf_op jit(solution)/shard_map/ppermute | solution.py:238
  29.3 9.6 %collective-permute-start.9 = (bf16[8,64,128]{2,1,0:T(8,128)(2,1)S(1)}, bf16[8,64,128]{2,1,0:T(8,128)(2,1)S(1)}, u32[]{:S(2)}, u32[]{:S(2)}) collective-permute-start(bf16[8,64,128]{2,1,0:T(8,128)(2,1)S(1)} %get-tuple-element.45), channel_id=1, source_target_pairs={{0,8},{8,0},{16,24},{24,16},{1,9},{9,1},{17,25},{25,17},{2,10},{10... | collective-permute-start | bytes 393224 | tf_op jit(solution)/shard_map/ppermute | solution.py:238
  29.8 7.2 %collective-permute-start.13 = (bf16[8,32,128]{2,1,0:T(8,128)(2,1)S(1)}, bf16[8,32,128]{2,1,0:T(8,128)(2,1)S(1)}, u32[]{:S(2)}, u32[]{:S(2)}) collective-permute-start(bf16[8,32,128]{2,1,0:T(8,128)(2,1)S(1)} %get-tuple-element.51), channel_id=1, source_target_pairs={{0,4},{1,5},{2,6},{3,7},{4,0},{5,1},{6,2},{7,3},{8,12},{9,13},{10,... | collective-permute-start | bytes 196616 | tf_op jit(solution)/shard_map/ppermute | solution.py:238
  29.8 16.0 %collective-permute-start.14 = (bf16[8,32,128]{2,1,0:T(8,128)(2,1)S(1)}, bf16[8,32,128]{2,1,0:T(8,128)(2,1)S(1)}, u32[]{:S(2)}, u32[]{:S(2)}) collective-permute-start(bf16[8,32,128]{2,1,0:T(8,128)(2,1)S(1)} %get-tuple-element.52), channel_id=1, source_target_pairs={{0,5},{1,4},{2,7},{3,6},{4,1},{5,0},{6,3},{7,2},{8,13},{9,12},{10,... | collective-permute-start | bytes 196616 | tf_op jit(solution)/shard_map/ppermute | solution.py:238
  37.0 11.2 %collective-permute-start.15 = (bf16[8,32,128]{2,1,0:T(8,128)(2,1)S(1)}, bf16[8,32,128]{2,1,0:T(8,128)(2,1)S(1)}, u32[]{:S(2)}, u32[]{:S(2)}) collective-permute-start(bf16[8,32,128]{2,1,0:T(8,128)(2,1)S(1)} %get-tuple-element.53), channel_id=1, source_target_pairs={{0,2},{1,3},{2,0},{3,1},{4,6},{5,7},{6,4},{7,5},{8,10},{9,11},{10,... | collective-permute-start | bytes 196616 | tf_op jit(solution)/shard_map/ppermute | solution.py:238
  37.0 11.2 %collective-permute-start.16 = (bf16[8,32,128]{2,1,0:T(8,128)(2,1)S(1)}, bf16[8,32,128]{2,1,0:T(8,128)(2,1)S(1)}, u32[]{:S(2)}, u32[]{:S(2)}) collective-permute-start(bf16[8,32,128]{2,1,0:T(8,128)(2,1)S(1)} %get-tuple-element.54), channel_id=1, source_target_pairs={{0,3},{1,2},{2,1},{3,0},{4,7},{5,6},{6,5},{7,4},{8,11},{9,10},{10,... | collective-permute-start | bytes 196616 | tf_op jit(solution)/shard_map/ppermute | solution.py:238
  37.0 11.2 %collective-permute-start.17 = (bf16[8,32,128]{2,1,0:T(8,128)(2,1)S(1)}, bf16[8,32,128]{2,1,0:T(8,128)(2,1)S(1)}, u32[]{:S(2)}, u32[]{:S(2)}) collective-permute-start(bf16[8,32,128]{2,1,0:T(8,128)(2,1)S(1)} %get-tuple-element.55), channel_id=1, source_target_pairs={{0,6},{1,7},{2,4},{3,5},{4,2},{5,3},{6,0},{7,1},{8,14},{9,15},{10,... | collective-permute-start | bytes 196616 | tf_op jit(solution)/shard_map/ppermute | solution.py:238
  38.9 9.3 %collective-permute-start.18 = (bf16[8,32,128]{2,1,0:T(8,128)(2,1)S(1)}, bf16[8,32,128]{2,1,0:T(8,128)(2,1)S(1)}, u32[]{:S(2)}, u32[]{:S(2)}) collective-permute-start(bf16[8,32,128]{2,1,0:T(8,128)(2,1)S(1)} %get-tuple-element.56), channel_id=1, source_target_pairs={{0,7},{1,6},{2,5},{3,4},{4,3},{5,2},{6,1},{7,0},{8,15},{9,14},{10,... | collective-permute-start | bytes 196616 | tf_op jit(solution)/shard_map/ppermute | solution.py:238
  45.8 24.3 %collective-permute-start.10 = (bf16[1040,128]{1,0:T(8,128)(2,1)S(1)}, bf16[1040,128]{1,0:T(8,128)(2,1)S(1)}, u32[]{:S(2)}, u32[]{:S(2)}) collective-permute-start(bf16[1040,128]{1,0:T(8,128)(2,1)S(1)} %get-tuple-element.47), channel_id=1, source_target_pairs={{0,16},{8,24},{16,0},{24,8},{1,17},{9,25},{17,1},{25,9},{2,18},{10... | collective-permute-start | bytes 798728 | tf_op jit(solution)/shard_map/ppermute | solution.py:238
  50.0 8.2 %collective-permute-start.19 = (bf16[8,64,128]{2,1,0:T(8,128)(2,1)S(1)}, bf16[8,64,128]{2,1,0:T(8,128)(2,1)S(1)}, u32[]{:S(2)}, u32[]{:S(2)}) collective-permute-start(bf16[8,64,128]{2,1,0:T(8,128)(2,1)S(1)} %get-tuple-element.57), channel_id=1, source_target_pairs={{0,16},{8,24},{16,0},{24,8},{1,17},{9,25},{17,1},{25,9},{2,18},{10... | collective-permute-start | bytes 393224 | tf_op jit(solution)/shard_map/ppermute | solution.py:238
  52.4 9.3 %collective-permute-start.20 = (bf16[8,64,128]{2,1,0:T(8,128)(2,1)S(1)}, bf16[8,64,128]{2,1,0:T(8,128)(2,1)S(1)}, u32[]{:S(2)}, u32[]{:S(2)}) collective-permute-start(bf16[8,64,128]{2,1,0:T(8,128)(2,1)S(1)} %get-tuple-element.58), channel_id=1, source_target_pairs={{0,24},{8,16},{16,8},{24,0},{1,25},{9,17},{17,9},{25,1},{2,26},{10... | collective-permute-start | bytes 393224 | tf_op jit(solution)/shard_map/ppermute | solution.py:238
  55.1 6.7 %collective-permute-start.21 = (bf16[8,64,128]{2,1,0:T(8,128)(2,1)S(1)}, bf16[8,64,128]{2,1,0:T(8,128)(2,1)S(1)}, u32[]{:S(2)}, u32[]{:S(2)}) collective-permute-start(bf16[8,64,128]{2,1,0:T(8,128)(2,1)S(1)} %get-tuple-element.59), channel_id=1, source_target_pairs={{0,8},{8,0},{16,24},{24,16},{1,9},{9,1},{17,25},{25,17},{2,10},{10... | collective-permute-start | bytes 393224 | tf_op jit(solution)/shard_map/ppermute | solution.py:238
  55.1 15.0 %collective-permute-start.11 = (bf16[1040,128]{1,0:T(8,128)(2,1)S(1)}, bf16[1040,128]{1,0:T(8,128)(2,1)S(1)}, u32[]{:S(2)}, u32[]{:S(2)}) collective-permute-start(bf16[1040,128]{1,0:T(8,128)(2,1)S(1)} %get-tuple-element.48), channel_id=1, source_target_pairs={{0,24},{8,16},{16,8},{24,0},{1,25},{9,17},{17,9},{25,1},{2,26},{10... | collective-permute-start | bytes 798728 | tf_op jit(solution)/shard_map/ppermute | solution.py:238
  58.2 15.0 %collective-permute-start.12 = (bf16[1040,128]{1,0:T(8,128)(2,1)S(1)}, bf16[1040,128]{1,0:T(8,128)(2,1)S(1)}, u32[]{:S(2)}, u32[]{:S(2)}) collective-permute-start(bf16[1040,128]{1,0:T(8,128)(2,1)S(1)} %get-tuple-element.49), channel_id=1, source_target_pairs={{0,8},{8,0},{16,24},{24,16},{1,9},{9,1},{17,25},{25,17},{2,10},{10... | collective-permute-start | bytes 798728 | tf_op jit(solution)/shard_map/ppermute | solution.py:238
  65.3 12.6 %collective-permute-start.23 = (bf16[1040,128]{1,0:T(8,128)(2,1)S(1)}, bf16[1040,128]{1,0:T(8,128)(2,1)S(1)}, u32[]{:S(2)}, u32[]{:S(2)}) collective-permute-start(bf16[1040,128]{1,0:T(8,128)(2,1)S(1)} %get-tuple-element.62), channel_id=1, source_target_pairs={{0,16},{8,24},{16,0},{24,8},{1,17},{9,25},{17,1},{25,9},{2,18},{10... | collective-permute-start | bytes 798728 | tf_op jit(solution)/shard_map/ppermute | solution.py:238
  68.5 11.1 %collective-permute-start.24 = (bf16[1040,128]{1,0:T(8,128)(2,1)S(1)}, bf16[1040,128]{1,0:T(8,128)(2,1)S(1)}, u32[]{:S(2)}, u32[]{:S(2)}) collective-permute-start(bf16[1040,128]{1,0:T(8,128)(2,1)S(1)} %get-tuple-element.63), channel_id=1, source_target_pairs={{0,24},{8,16},{16,8},{24,0},{1,25},{9,17},{17,9},{25,1},{2,26},{10... | collective-permute-start | bytes 798728 | tf_op jit(solution)/shard_map/ppermute | solution.py:238
  70.0 12.8 %collective-permute-start.22 = (bf16[1040,128]{1,0:T(8,128)(2,1)S(1)}, bf16[1040,128]{1,0:T(8,128)(2,1)S(1)}, u32[]{:S(2)}, u32[]{:S(2)}) collective-permute-start(bf16[1040,128]{1,0:T(8,128)(2,1)S(1)} %get-tuple-element.61), channel_id=1, source_target_pairs={{0,8},{8,0},{16,24},{24,16},{1,9},{9,1},{17,25},{25,17},{2,10},{10... | collective-permute-start | bytes 798728 | tf_op jit(solution)/shard_map/ppermute | solution.py:238
  (3 other events, 47.8 us)
